TPU v7x, 32 devices: a whole 2x2x4 slice. The times are simulated.
32 devices in a mesh: seq: 16 (over z, y, core), exp: 2 (over x).
Axes of the slice: x: 2, y: 2, z: 4, core: 2. Of those that a mesh axis runs over, the one named last changes fastest.
Arguments:
- hidden_in: bfloat16 [6, 6144], P('exp', 'seq'), may hold values from -2 to 2
- queries: bfloat16 [6, 6144], P(None, 'exp'), may hold values from -40 to 40
- key_cache: bfloat16 [6, 8192, 1024], P(None, 'seq', 'exp'), may hold values from -16 to 16
- value_cache: bfloat16 [6, 8192, 1024], P(None, 'seq', 'exp'), may hold values from -6 to 6
- lengths: int32 [6], replicated, may hold values from 2 to 8192
- out_weight: bfloat16 [6144, 6144], P('exp', 'seq'), may hold values from -0.078125 to 0.078125
- norm_gain: float32 [6144], P('seq'), may hold values from 0.1 to 1.9
- router: bfloat16 [6144, 8], P('seq'), may hold values from -0.078125 to 0.078125
- expert_ids: int32 [6, 2], P('exp'), may hold values from 0 to 7, as said below
- capacity: int32 [8], replicated, may hold values from 1 to 3, as said below
- w_gate: bfloat16 [8, 6144, 8192], P('exp', None, 'seq'), may hold values from -0.078125 to 0.078125
- w_up: bfloat16 [8, 6144, 8192], P('exp', None, 'seq'), may hold values from -0.078125 to 0.078125
- w_down: bfloat16 [8, 8192, 6144], P('exp', 'seq'), may hold values from -0.09375 to 0.09375
Outputs:
- layer_out: bfloat16 [6, 6144], P('exp', 'seq')
Inputs may be any that keep to these rules, and one draw needn't show every extreme that they name: lengths[b] counts sequence b's live cache positions, the newest token's included. `expert_ids`: the two experts of a token differ. One expert is named by every token; any other expert is named at most 3 times within one aligned block of 3 tokens. The expert that every token names has capacity 3.
All inputs are finite; a program needn't handle non-finite values.
Results may differ from a plain program's by a relative error of at most 0.0085.
Values may be sent and summed in bfloat16 or wider, within the bound.
A program may use at most 128 MiB of HBM per device.

v0:
```python
import functools
import math

import jax
import jax.numpy as jnp
from jax import lax
from jax.experimental import pallas as pl
from jax.experimental.pallas import tpu as pltpu
from jax.sharding import PartitionSpec as P

MESH = pl.DeviceIdType.MESH
HEAD_DIM = 128
LANES = 128
masked_score = -1e30
norm_eps = 1e-05
F32 = jnp.float32
BF16 = jnp.bfloat16


def up(value, step):
    return -(-value // step) * step


def iota(shape, axis):
    return lax.broadcasted_iota(jnp.int32, shape, axis)


def div(value, by):
    return lax.div(value, jnp.full_like(value, by))


def rem(value, by):
    return lax.rem(value, jnp.full_like(value, by))


def dot(a, b):
    return jnp.dot(a, b, preferred_element_type=F32)


def attend_kernel(len_ref, q_ref, k_ref, v_ref, o_ref):
    b = pl.program_id(0)
    span = k_ref.shape[1]
    kvl, gp = q_ref.shape[1], q_ref.shape[2]
    first = lax.axis_index("seq") * span
    live = (iota((gp, span), 1) + first) < len_ref[b]
    lane = iota((gp, LANES), 1)
    for kv in range(kvl):
        cols = slice(kv * HEAD_DIM, (kv + 1) * HEAD_DIM)
        s = lax.dot_general(
            q_ref[0, kv], k_ref[0, :, cols], (((1,), (1,)), ((), ())), preferred_element_type=F32
        ) * (1.0 / math.sqrt(HEAD_DIM))
        s = jnp.where(live, s, masked_score)
        m = jnp.max(s, axis=1, keepdims=True).astype(BF16).astype(F32)
        w = jnp.where(live, jnp.exp(s - m), 0.0)
        l = jnp.sum(w, axis=1, keepdims=True)
        acc = dot(w.astype(BF16), v_ref[0, :, cols])
        l_hi = l.astype(BF16).astype(F32)
        stats = jnp.where(lane == 0, m, jnp.where(lane == 1, l_hi, jnp.where(lane == 2, l - l_hi, 0.0)))
        rows = slice(kv * gp, (kv + 1) * gp)
        o_ref[rows, :HEAD_DIM] = acc.astype(BF16)
        o_ref[rows, HEAD_DIM:] = stats.astype(BF16)


def ring_of(axis, count):
    me = lax.axis_index(axis)
    return me, [lax.rem(me + k, count) for k in range(count)], [lax.rem(me + count - k, count) for k in range(count)]


def merge_kernel(
    dims, x_ref, ids_ref, ow_hbm, hid_ref, gain_ref, rt_ref,
    xg_ref, st_ref, idv_ref, res_ref,
    ow, send1, recv1, buf2, buf3, buf4,
    ow_sem, ss1, rs1, ss2, rs2, ss3, rs3, ss4, rs4,
):
    n_seq, n_exp, seqs, toks, kvl, group, rv, rp = dims
    gp = up(group, 8)
    heads = kvl * group
    bp = buf3.shape[1]
    width = hid_ref.shape[1]
    me, to_seq, from_seq = ring_of("seq", n_seq)
    my_e, to_exp, from_exp = ring_of("exp", n_exp)

    barrier = pltpu.get_barrier_semaphore()
    for k in range(1, n_seq):
        pl.semaphore_signal(barrier, inc=1, device_id={"seq": to_seq[k]}, device_id_type=MESH)
    for k in range(1, n_exp):
        pl.semaphore_signal(barrier, inc=1, device_id={"exp": to_exp[k]}, device_id_type=MESH)
    ow_copy = pltpu.make_async_copy(ow_hbm, ow, ow_sem)
    ow_copy.start()

    src = iota((1, x_ref.shape[0]), 1)
    src_h = rem(src, kvl * gp)
    src_g = rem(src_h, gp)
    src_row = div(src, kvl * gp) * heads + div(src_h, gp) * group + src_g
    src_row = jnp.where(src_g < group, src_row, -1)
    slot = iota((n_seq * rp, 1), 0)
    slot_k = rem(slot, rp)
    slot_row = jnp.where(slot_k < rv, div(slot, rp) * rv + slot_k, -2)
    pack = (slot_row == src_row).astype(F32).astype(BF16)
    packed = dot(pack, x_ref[...]).astype(BF16)
    for p in range(n_seq):
        send1[p] = packed[p * rp:(p + 1) * rp]
    recv1[me] = send1[me]
    pl.semaphore_wait(barrier, n_seq + n_exp - 2)

    out1 = []
    for k in range(1, n_seq):
        c = pltpu.make_async_remote_copy(
            send1.at[to_seq[k]], recv1.at[me], ss1.at[k], rs1.at[k],
            device_id={"seq": to_seq[k]}, device_id_type=MESH)
        c.start()
        out1.append(c)
    for k in range(1, n_seq):
        pltpu.make_async_remote_copy(
            send1.at[to_seq[k]], recv1.at[from_seq[k]], ss1.at[k], rs1.at[k],
            device_id={"seq": to_seq[k]}, device_id_type=MESH).wait_recv()
    stats = [recv1[p][:, HEAD_DIM:].astype(F32) for p in range(n_seq)]
    peaks = [s[:, 0:1] for s in stats]
    top = functools.reduce(jnp.maximum, peaks)
    acc = jnp.zeros((rp, HEAD_DIM), F32)
    den = jnp.zeros((rp, 1), F32)
    for p in range(n_seq):
        f = jnp.exp(peaks[p] - top)
        den = den + (stats[p][:, 1:2] + stats[p][:, 2:3]) * f
        acc = acc + recv1[p][:, :HEAD_DIM].astype(F32) * f
    att = jnp.where(den > 0.0, acc / jnp.where(den > 0.0, den, 1.0), 0.0)
    buf2[me] = att.astype(BF16)

    def gather(buf, sends, recvs, axis, mine, to, frm):
        started = []
        for k in range(1, len(to)):
            c = pltpu.make_async_remote_copy(
                buf.at[mine], buf.at[mine], sends.at[k], recvs.at[k],
                device_id={axis: to[k]}, device_id_type=MESH)
            c.start()
            started.append(c)
        for k in range(1, len(to)):
            pltpu.make_async_remote_copy(
                buf.at[mine], buf.at[frm[k]], sends.at[k], recvs.at[k],
                device_id={axis: to[k]}, device_id_type=MESH).wait_recv()
        return started

    out2 = gather(buf2, ss2, rs2, "seq", me, to_seq, from_seq)
    row = iota((heads * bp, 1), 0)
    row_b = rem(row, bp)
    want = jnp.where(row_b < seqs, row_b * heads + div(row, bp), -3)
    slot = iota((1, n_seq * rp), 1)
    slot_k = rem(slot, rp)
    have = jnp.where(slot_k < rv, div(slot, rp) * rv + slot_k, -2)
    unpack = (want == have).astype(F32).astype(BF16)
    rows = dot(unpack, jnp.concatenate([buf2[p] for p in range(n_seq)], axis=0))
    att_all = jnp.concatenate([rows[h * bp:(h + 1) * bp] for h in range(heads)], axis=1).astype(BF16)
    ow_copy.wait()
    part = dot(att_all, ow[...])
    hid = hid_ref[...].astype(F32)
    rowc = iota((bp, width), 0)
    rowl = iota((bp, LANES), 0)
    lane = iota((bp, LANES), 1)
    idv = jnp.zeros((bp, LANES), F32)
    for t in range(toks):
        at = my_e * toks + t
        part = part + jnp.where(rowc == at, hid[t:t + 1, :], 0.0)
        for k in range(2):
            idv = idv + jnp.where((rowl == at) & (lane == k), ids_ref[t, k].astype(F32), 0.0)
    buf3[my_e, :, :width] = part
    buf3[my_e, :, width:] = idv
    out3 = gather(buf3, ss3, rs3, "exp", my_e, to_exp, from_exp)
    total = functools.reduce(lambda a, b: a + b, [buf3[e] for e in range(n_exp)])
    residual = total[:, :width]
    idv_ref[...] = total[:, width:].astype(jnp.int32)
    for t in range(toks):
        mine = jnp.sum(jnp.where(rowc == my_e * toks + t, residual, 0.0), axis=0, keepdims=True)
        res_ref[t:t + 1, :] = mine
    gained = residual * gain_ref[...]
    logit = jnp.dot(gained, rt_ref[...].astype(F32), precision=lax.Precision.HIGHEST, preferred_element_type=F32)
    square = jnp.sum(residual * residual, axis=1, keepdims=True)
    st = jnp.where(lane == 15, square, logit)
    hi = st.astype(BF16).astype(F32)
    buf4[me, :, :width] = gained.astype(BF16)
    buf4[me, :, width:] = (hi + pltpu.roll(st - hi, 16, 1)).astype(BF16)
    out4 = gather(buf4, ss4, rs4, "seq", me, to_seq, from_seq)
    tot = jnp.zeros((bp, LANES), F32)
    for p in range(n_seq):
        xg_ref[:, p * width:(p + 1) * width] = buf4[p, :, :width]
        tot = tot + buf4[p, :, width:].astype(F32)
    st_ref[...] = tot + pltpu.roll(tot, LANES - 16, 1)
    for c in out1 + out2 + out3 + out4:
        c.wait_send()


def expert_kernel(
    dims, ids_ref, cap_ref, xg_ref, st_ref, idv_ref, wg_hbm, wu_hbm, wd_hbm,
    o_ref, gate, upb, down, y, coef, order, sems,
):
    n_seq, n_exp, seqs, toks, n_experts, chunk = dims
    local = wg_hbm.shape[0]
    bp, model = xg_ref.shape
    width = model // n_seq
    slots = gate.shape[0]
    chunks = wg_hbm.shape[2] // chunk
    first = lax.axis_index("exp") * local

    count = jnp.int32(0)
    for e in range(local):
        named = jnp.int32(0)
        for b in range(seqs):
            for k in range(2):
                named = named | (ids_ref[b, k] == first + e).astype(jnp.int32)

        @pl.when(named > 0)
        def _():
            order[count] = e

        count = count + named
    steps = count * chunks

    def copies(i):
        s = lax.rem(i, slots)
        e = order[lax.div(i, chunks)]
        at = pl.multiple_of(lax.rem(i, chunks) * chunk, chunk)
        return (
            pltpu.make_async_copy(wg_hbm.at[e, :, pl.ds(at, chunk)], gate.at[s], sems.at[s, 0]),
            pltpu.make_async_copy(wu_hbm.at[e, :, pl.ds(at, chunk)], upb.at[s], sems.at[s, 1]),
            pltpu.make_async_copy(wd_hbm.at[e, pl.ds(at, chunk), :], down.at[s], sems.at[s, 2]),
        )

    for i in range(slots - 1):
        @pl.when(i < steps)
        def _():
            for c in copies(jnp.int32(i)):
                c.start()

    st = st_ref[...]
    lane = iota((bp, LANES), 1)
    rowc = iota((bp, 1), 0)
    scale = lax.rsqrt(st[:, 15:16] / model + norm_eps)
    logits = jnp.where(lane < n_experts, st, 0.0) * scale
    ids = [idv_ref[:, k:k + 1] for k in range(2)]
    chosen = [jnp.sum(jnp.where(lane == ids[k], logits, 0.0), axis=1, keepdims=True) for k in range(2)]
    weight = []
    for k in range(2):
        rank = jnp.zeros((bp, 1), jnp.int32)
        for b in range(seqs):
            end = (b // toks + 1) * toks
            later = (rowc > b) & (rowc < end)
            for j in range(2):
                rank = rank + jnp.where(later & (ids[k] == ids_ref[b, j]), 1, 0)
        limit = jnp.zeros((bp, 1), jnp.int32)
        for e in range(n_experts):
            limit = limit + jnp.where(ids[k] == e, cap_ref[e], 0)
        keep = (rank < limit) & (rowc < seqs)
        weight.append(jnp.where(keep, jax.nn.sigmoid(chosen[k] - chosen[1 - k]), 0.0))
    coef[0] = jnp.broadcast_to(weight[0], (bp, LANES))
    coef[1] = jnp.broadcast_to(weight[1], (bp, LANES))
    y[...] = jnp.zeros_like(y)

    def step(i, carry):
        for c in copies(i):
            c.wait()

        @pl.when(i + slots - 1 < steps)
        def _():
            for c in copies(i + slots - 1):
                c.start()

        s = lax.rem(i, slots)
        e = order[lax.div(i, chunks)] + first
        x = xg_ref[...]
        g = dot(x, gate[s]) * scale
        u = dot(x, upb[s]) * scale
        h = (jax.nn.silu(g) * u).astype(BF16)
        c = jnp.where(ids[0] == e, coef[0][:, :1], 0.0) + jnp.where(ids[1] == e, coef[1][:, :1], 0.0)
        y[...] += dot(h, down[s]) * c
        return carry

    lax.fori_loop(0, steps, step, jnp.int32(0))
    for e in range(n_exp):
        rows = y[e * toks:(e + 1) * toks, :].astype(BF16)
        for s in range(n_seq):
            o_ref[e * n_seq + s] = rows[:, s * width:(s + 1) * width]


def scatter_kernel(dims, y_ref, res_ref, o_ref, recv, ss, rs):
    n_seq, n_exp = dims
    n = n_seq * n_exp
    me = lax.axis_index("exp") * n_seq + lax.axis_index("seq")
    to = [lax.rem(me + k, n) for k in range(n)]
    frm = [lax.rem(me + n - k, n) for k in range(n)]

    def where(p):
        return {"seq": lax.rem(p, n_seq), "exp": lax.div(p, n_seq)}

    barrier = pltpu.get_barrier_semaphore()
    for k in range(1, n):
        pl.semaphore_signal(barrier, inc=1, device_id=where(to[k]), device_id_type=MESH)
    recv[me] = y_ref[me]
    pl.semaphore_wait(barrier, n - 1)
    started = []
    for k in range(1, n):
        c = pltpu.make_async_remote_copy(
            y_ref.at[to[k]], recv.at[me], ss.at[k], rs.at[k],
            device_id=where(to[k]), device_id_type=MESH)
        c.start()
        started.append(c)
    for k in range(1, n):
        pltpu.make_async_remote_copy(
            y_ref.at[to[k]], recv.at[frm[k]], ss.at[k], rs.at[k],
            device_id=where(to[k]), device_id_type=MESH).wait_recv()
    total = res_ref[...]
    for p in range(n):
        total = total + recv[p].astype(F32)
    o_ref[...] = total.astype(BF16)
    for c in started:
        c.wait_send()


def on_device(
    n_seq, n_exp, hidden_in, queries, key_cache, value_cache, lengths, out_weight, norm_gain,
    router, expert_ids, capacity, w_gate, w_up, w_down,
):
    seqs = queries.shape[0]
    toks, width = hidden_in.shape
    span = key_cache.shape[1]
    kvl = key_cache.shape[2] // HEAD_DIM
    heads = queries.shape[1] // HEAD_DIM
    group = heads // kvl
    gp = up(group, 8)
    bp = up(seqs, 8)
    n_experts = router.shape[1]
    model = width * n_seq
    rv = -(-seqs * heads // n_seq)
    rp = up(rv, 16)
    vmem = pl.BlockSpec(memory_space=pltpu.VMEM)
    smem = pl.BlockSpec(memory_space=pltpu.SMEM)
    hbm = pl.BlockSpec(memory_space=pltpu.HBM)
    q = jnp.pad(queries.reshape(seqs, kvl, group, HEAD_DIM), ((0, 0), (0, 0), (0, gp - group), (0, 0)))
    partial = pl.pallas_call(
        attend_kernel,
        grid=(seqs,),
        in_specs=[
            smem,
            pl.BlockSpec((1, kvl, gp, HEAD_DIM), lambda b: (b, 0, 0, 0)),
            pl.BlockSpec((1, span, kvl * HEAD_DIM), lambda b: (b, 0, 0)),
            pl.BlockSpec((1, span, kvl * HEAD_DIM), lambda b: (b, 0, 0)),
        ],
        out_specs=pl.BlockSpec((kvl * gp, 2 * HEAD_DIM), lambda b: (b, 0)),
        out_shape=jax.ShapeDtypeStruct((seqs * kvl * gp, 2 * HEAD_DIM), BF16),
        name="attend",
    )(lengths, q, key_cache, value_cache)

    dma = pltpu.SemaphoreType.DMA
    rt = jnp.pad(router, ((0, 0), (0, LANES - n_experts)))
    xg, st, idv, res = pl.pallas_call(
        functools.partial(merge_kernel, (n_seq, n_exp, seqs, toks, kvl, group, rv, rp)),
        in_specs=[vmem, smem, hbm, vmem, vmem, vmem],
        out_specs=[vmem] * 4,
        out_shape=[
            jax.ShapeDtypeStruct((bp, model), BF16),
            jax.ShapeDtypeStruct((bp, LANES), F32),
            jax.ShapeDtypeStruct((bp, LANES), jnp.int32),
            jax.ShapeDtypeStruct((toks, width), F32),
        ],
        scratch_shapes=[
            pltpu.VMEM(out_weight.shape, BF16),
            pltpu.VMEM((n_seq, rp, 2 * HEAD_DIM), BF16),
            pltpu.VMEM((n_seq, rp, 2 * HEAD_DIM), BF16),
            pltpu.VMEM((n_seq, rp, HEAD_DIM), BF16),
            pltpu.VMEM((n_exp, bp, width + LANES), F32),
            pltpu.VMEM((n_seq, bp, width + LANES), BF16),
            dma,
            dma((n_seq,)), dma((n_seq,)), dma((n_seq,)), dma((n_seq,)),
            dma((n_exp,)), dma((n_exp,)), dma((n_seq,)), dma((n_seq,)),
        ],
        compiler_params=pltpu.CompilerParams(collective_id=0, has_side_effects=True),
        name="merge",
    )(partial, expert_ids, out_weight, hidden_in, norm_gain.reshape(1, width), rt)

    chunk = min(256, w_gate.shape[2])
    slots = 3
    y = pl.pallas_call(
        functools.partial(expert_kernel, (n_seq, n_exp, seqs, toks, n_experts, chunk)),
        in_specs=[smem, smem, vmem, vmem, vmem, hbm, hbm, hbm],
        out_specs=vmem,
        out_shape=jax.ShapeDtypeStruct((n_exp * n_seq, toks, width), BF16),
        scratch_shapes=[
            pltpu.VMEM((slots, model, chunk), BF16),
            pltpu.VMEM((slots, model, chunk), BF16),
            pltpu.VMEM((slots, chunk, model), BF16),
            pltpu.VMEM((bp, model), F32),
            pltpu.VMEM((2, bp, LANES), F32),
            pltpu.SMEM((w_gate.shape[0],), jnp.int32),
            dma((slots, 3)),
        ],
        compiler_params=pltpu.CompilerParams(vmem_limit_bytes=48 * 1024 * 1024),
        name="experts",
    )(idv, capacity, xg, st, idv, w_gate, w_up, w_down)

    return pl.pallas_call(
        functools.partial(scatter_kernel, (n_seq, n_exp)),
        in_specs=[vmem, vmem],
        out_specs=vmem,
        out_shape=jax.ShapeDtypeStruct((toks, width), BF16),
        scratch_shapes=[
            pltpu.VMEM((n_exp * n_seq, toks, width), BF16),
            dma((n_exp * n_seq,)), dma((n_exp * n_seq,)),
        ],
        compiler_params=pltpu.CompilerParams(collective_id=1, has_side_effects=True),
        name="scatter",
    )(y, res)


def solution(mesh):
    in_specs = (
        P("exp", "seq"),
        P(None, "exp"),
        P(None, "seq", "exp"),
        P(None, "seq", "exp"),
        P(),
        P("exp", "seq"),
        P("seq"),
        P("seq", None),
        P("exp", None),
        P(),
        P("exp", None, "seq"),
        P("exp", None, "seq"),
        P("exp", "seq", None),
    )
    return jax.shard_map(
        functools.partial(on_device, mesh.shape["seq"], mesh.shape["exp"]),
        mesh=mesh, in_specs=in_specs, out_specs=P("exp", "seq"), check_vma=False,
    )
```

profile of v0, /device:TPU:0, one launch (start us, length us, event | category | flops | bytes accessed | tf_op | source)
XLA Modules:
  0.0 73.8 jit_solution(14269819786556644987)
XLA Ops:
  0.0 1.3 %reshape.7.gain_ref = f32[1,384]{1,0:T(1,128)} reshape(f32[384]{0:T(512)} %param.19) | data formatting | bytes 3072 | tf_op jit(solution)/shard_map/reshape | solution.py:376
  1.3 1.3 %copy.17.ids_ref = s32[3,2]{1,0:T(4,128)} copy(s32[3,2]{0,1:T(2,128)} %param.21) | data formatting | bytes 48 | tf_op args[8]
  2.6 0.9 %reshape.6 = bf16[6,4,6,128]{3,2,1,0:T(8,128)(2,1)S(1)} reshape(bf16[6,3072]{1,0:T(8,128)(2,1)} %param.14) | data formatting | bytes 73728 | tf_op jit(solution)/shard_map/reshape | solution.py:336
  3.5 0.6 pad.8.q_ref
  4.1 8.7 %attend.1.x_ref = bf16[192,256]{1,0:T(8,128)(2,1)} custom-call(s32[6]{0:T(128)} %len_ref.1, bf16[6,4,8,128]{3,2,1,0:T(8,128)(2,1)} %pad.8.q_ref, bf16[6,512,512]{2,1,0:T(8,128)(2,1)} %k_ref.1, bf16[6,512,512]{2,1,0:T(8,128)(2,1)} %v_ref.1), custom_call_target="tpu_custom_call" | custom-call | tf_op jit(solution)/shard_map/attend/pallas_call | solution.py:337
  12.8 0.8 %copy.16 = bf16[384,8]{1,0:T(8,128)(2,1)S(1)} copy(bf16[384,8]{0,1:T(8,128)(2,1)} %param.20) | data formatting | bytes 12288 | tf_op args[7]
  13.6 0.7 pad.9.rt_ref
  14.3 25.5 %merge.1 = (bf16[8,6144]{1,0:T(8,128)(2,1)}, f32[8,128]{1,0:T(8,128)}, s32[8,128]{1,0:T(8,128)}, f32[3,384]{1,0:T(4,128)}) custom-call(bf16[192,256]{1,0:T(8,128)(2,1)} %attend.1.x_ref, s32[3,2]{1,0:T(4,128)} %copy.17.ids_ref, bf16[3072,384]{1,0:T(8,128)(2,1)} %ow_hbm.1, bf16[3,384]{1,0:T(4,128)(2,1)} %hid_ref.1, f32[1,384]{1,0:T(1,128)} %reshape.7.gain_ref, ...), custom_call_target="tpu_custom_call" | custom-call | tf_op jit(solution)/shard_map/merge/pallas_call | solution.py:353
  39.7 0.0 copy-start.1
  39.8 0.9 %copy-done.1 = bf16[8,6144]{1,0:T(8,128)(2,1)S(1)} copy-done((bf16[8,6144]{1,0:T(8,128)(2,1)S(1)}, bf16[8,6144]{1,0:T(8,128)(2,1)}, u32[]{:S(2)}) %copy-start.1) | copy-done | bytes 98328
  40.6 0.0 copy-start.2
  40.6 0.7 copy-done.2
  41.3 0.0 copy-start.3
  41.3 0.7 copy-done.3
  42.0 0.0 copy-start.4
  42.0 0.7 copy-done.4
  42.6 14.2 %experts.1.y_ref = bf16[32,3,384]{2,1,0:T(4,128)(2,1)S(1)} custom-call(s32[8,128]{1,0:T(8,128)S(1)} %copy-done.2, s32[8]{0:T(128)S(1)} %copy-done.4, bf16[8,6144]{1,0:T(8,128)(2,1)S(1)} %copy-done.1, f32[8,128]{1,0:T(8,128)S(1)} %copy-done.3, s32[8,128]{1,0:T(8,128)S(1)} %copy-done.2, bf16[4,6144,512]{2,1,0:T(8,128)(2,1)} %wg_hbm.1, ...), custom_call_target="tpu_custom_call" | custom-call | tf_op jit(solution)/shard_map/experts/pallas_call | solution.py:380
  56.9 0.0 copy-start
  56.9 0.6 copy-done
  57.5 15.1 %scatter.1 = bf16[3,384]{1,0:T(4,128)(2,1)} custom-call(bf16[32,3,384]{2,1,0:T(4,128)(2,1)} %copy-done, f32[3,384]{1,0:T(4,128)} %get-tuple-element.12.res_ref), custom_call_target="tpu_custom_call" | custom-call | tf_op jit(solution)/shard_map/scatter/pallas_call | solution.py:398
  72.6 1.2 %copy.19 = bf16[3,384]{1,0:T(4,128)(2,1)} copy(bf16[3,384]{1,0:T(4,128)(2,1)} %scatter.1) | data formatting | bytes 4608
Async XLA Ops:
  39.7 0.9 %copy-start.1 = (bf16[8,6144]{1,0:T(8,128)(2,1)S(1)}, bf16[8,6144]{1,0:T(8,128)(2,1)}, u32[]{:S(2)}) copy-start(bf16[8,6144]{1,0:T(8,128)(2,1)} %get-tuple-element.10.xg_ref) | copy-start | bytes 294916
  40.6 0.7 copy-start.2
  41.3 0.7 copy-start.3
  42.0 0.7 copy-start.4
  56.9 0.6 copy-start
where the time goes:
time: 74.6 us; the launch traced here: 73.8 us
  Pallas kernels  63.4 us (85%)
  local copies, waits for them, and re-layouts  10.4 us (14%)
    pallas_call x1, Pallas kernels, on_device(): pl.pallas_call(functools.partial(merge_kernel, (n_seq, n_exp, seqs, toks,...  25.5 us
    pallas_call x1, Pallas kernels, on_device(): pl.pallas_call(functools.partial(scatter_kernel, (n_seq, n_exp)), in_spec...  15.1 us
    pallas_call x1, Pallas kernels, on_device(): pl.pallas_call(functools.partial(expert_kernel, (n_seq, n_exp, seqs, toks...  14.2 us
    pallas_call x1, Pallas kernels, on_device(): pl.pallas_call(attend_kernel, grid=(seqs,), in_specs=[smem, pl.BlockSpec(...  8.66 us
    unnamed x13, local copies, waits for them, and re-layouts  6.95 us

commit v1 on v0

v1 whole, which is shorter than its diff:
```python
import functools
import math

import jax
import jax.numpy as jnp
from jax import lax
from jax.experimental import pallas as pl
from jax.experimental.pallas import tpu as pltpu
from jax.sharding import PartitionSpec as P

MESH = pl.DeviceIdType.MESH
HEAD_DIM = 128
LANES = 128
VMEM_BYTES = 67043328
masked_score = -1e30
norm_eps = 1e-05
F32 = jnp.float32
BF16 = jnp.bfloat16


def up(value, step):
    return -(-value // step) * step


def iota(shape, axis):
    return lax.broadcasted_iota(jnp.int32, shape, axis)


def div(value, by):
    return lax.div(value, jnp.full_like(value, by))


def rem(value, by):
    return lax.rem(value, jnp.full_like(value, by))


def dot(a, b):
    return jnp.dot(a, b, preferred_element_type=F32)


def dot_nt(a, b):
    return lax.dot_general(a, b, (((1,), (1,)), ((), ())), preferred_element_type=F32)


def ring_of(axis, count):
    me = lax.axis_index(axis)
    return me, [lax.rem(me + k, count) for k in range(count)], [lax.rem(me + count - k, count) for k in range(count)]


def weight_order(local):
    order = []
    for e in range(local):
        order += [("gate", e), ("up", e)]
        if e:
            order.append(("down", e - 1))
    return order + [("down", local - 1)]


def layer_kernel(
    dims, len_ref, cap_ref, ids_ref,
    hid_hbm, q_hbm, k_hbm, v_hbm, ow_hbm, gain_hbm, rt_hbm, wg_hbm, wu_hbm, wd_hbm,
    o_ref,
    hid, qv, kbuf, vbuf, ow, gain, rt, pool,
    qs, pk, sk, unpk, send1, recv1, buf2, buf3, idx, buf4, st4, xg, y, ysend, yrecv,
    in_sem, kv_sem, w_sem, ss1, rs1, ss2, rs2, ss3, rs3, ssi, rsi, ss4, rs4, sst, rst, ss5, rs5,
):
    n_seq, n_exp, seqs, toks, kvl, group, rv, rp, n_experts, slots = dims
    heads = kvl * group
    span = kbuf.shape[1]
    bp = y.shape[0]
    model = y.shape[1]
    width = model // n_seq
    local, ffl = wg_hbm.shape[0], wg_hbm.shape[2]
    n = n_seq * n_exp
    me, to_seq, from_seq = ring_of("seq", n_seq)
    my_e, to_exp, from_exp = ring_of("exp", n_exp)
    me_all = my_e * n_seq + me
    to_all = [lax.rem(me_all + k, n) for k in range(n)]
    from_all = [lax.rem(me_all + n - k, n) for k in range(n)]

    def where_is(p):
        return {"seq": lax.rem(p, n_seq), "exp": lax.div(p, n_seq)}

    barrier = pltpu.get_barrier_semaphore()
    for k in range(1, n):
        pl.semaphore_signal(barrier, inc=1, device_id=where_is(to_all[k]), device_id_type=MESH)

    q_copy = pltpu.make_async_copy(q_hbm, qv, in_sem.at[0])
    q_copy.start()
    kv_copies = []
    for b in range(seqs):
        pair = (
            pltpu.make_async_copy(k_hbm.at[b], kbuf.at[b], kv_sem.at[b, 0]),
            pltpu.make_async_copy(v_hbm.at[b], vbuf.at[b], kv_sem.at[b, 1]),
        )
        for c in pair:
            c.start()
        kv_copies.append(pair)
    small = [
        pltpu.make_async_copy(hid_hbm, hid, in_sem.at[1]),
        pltpu.make_async_copy(gain_hbm, gain.at[0], in_sem.at[2]),
        pltpu.make_async_copy(rt_hbm, rt, in_sem.at[3]),
    ]
    ow_copy = pltpu.make_async_copy(ow_hbm, ow, in_sem.at[4])
    for c in small + [ow_copy]:
        c.start()

    order = weight_order(local)

    def weight_copies(i):
        kind, e = order[i]
        s = i % slots
        if kind == "gate":
            return [pltpu.make_async_copy(wg_hbm.at[e], pool.at[s], w_sem.at[i])]
        if kind == "up":
            return [pltpu.make_async_copy(wu_hbm.at[e], pool.at[s], w_sem.at[i])]
        return [
            pltpu.make_async_copy(
                wd_hbm.at[e, :, pl.ds(j * ffl, ffl)], pool.at[s, pl.ds(j * ffl, ffl), :], w_sem.at[i])
            for j in range(model // ffl)
        ]

    def weight_wait(i):
        s = i % slots
        pltpu.make_async_copy(wg_hbm.at[0], pool.at[s], w_sem.at[i]).wait()

    for i in range(min(slots, len(order))):
        for c in weight_copies(i):
            c.start()

    pk[...] = jnp.zeros_like(pk)
    sk[...] = jnp.zeros_like(sk)
    qs[...] = jnp.zeros_like(qs)
    row = iota((heads * bp, 1), 0)
    row_b = rem(row, bp)
    want = jnp.where(row_b < seqs, row_b * heads + div(row, bp), -3)
    slot = iota((1, n_seq * rp), 1)
    slot_k = rem(slot, rp)
    have = jnp.where(slot_k < rv, div(slot, rp) * rv + slot_k, -2)
    unpk[...] = (want == have).astype(F32).astype(BF16)

    rowl = iota((bp, LANES), 0)
    lane = iota((bp, LANES), 1)
    mine = jnp.zeros((bp, LANES), F32)
    for t in range(toks):
        for k in range(2):
            mine = mine + jnp.where((rowl == my_e * toks + t) & (lane == k), ids_ref[k, t].astype(F32), 0.0)
    idx[my_e] = mine

    q_copy.wait()
    for h in range(heads):
        qs[h * bp:h * bp + seqs, :] = qv[:, h * HEAD_DIM:(h + 1) * HEAD_DIM].astype(F32)

    pl.semaphore_wait(barrier, n - 1)

    def send(src, dst, send_sem, recv_sem, device):
        c = pltpu.make_async_remote_copy(src, dst, send_sem, recv_sem, device_id=device, device_id_type=MESH)
        c.start()
        return c

    def spread(buf, sends, recvs, axis, mine_at, to):
        return [send(buf.at[mine_at], buf.at[mine_at], sends.at[k], recvs.at[k], {axis: to[k]}) for k in range(1, len(to))]

    def collect(buf, sends, recvs, axis, mine_at, to, frm):
        for k in range(1, len(to)):
            pltpu.make_async_remote_copy(
                buf.at[mine_at], buf.at[frm[k]], sends.at[k], recvs.at[k],
                device_id={axis: to[k]}, device_id_type=MESH).wait_recv()

    started = spread(idx, ssi, rsi, "exp", my_e, to_exp)

    first = me * span
    pos = iota((heads, span), 1) + first
    hrow = iota((heads, 1), 0)
    kv_of = div(hrow, group)
    diag = div(iota((heads, kvl * HEAD_DIM), 1), HEAD_DIM) == kv_of
    lane_h = iota((heads, LANES), 1)
    for b in range(seqs):
        qb = qs[pl.ds(b, heads, stride=bp), :]
        qd = jnp.where(diag, jnp.concatenate([qb] * kvl, axis=1), 0.0).astype(BF16)
        for c in kv_copies[b]:
            c.wait()
        live = pos < len_ref[b]
        s = jnp.where(live, dot_nt(qd, kbuf[b]) * (1.0 / math.sqrt(HEAD_DIM)), masked_score)
        m = jnp.max(s, axis=1, keepdims=True).astype(BF16).astype(F32)
        w = jnp.where(live, jnp.exp(s - m), 0.0)
        l = jnp.sum(w, axis=1, keepdims=True)
        wide = dot(w.astype(BF16), vbuf[b])
        acc = jnp.zeros((heads, HEAD_DIM), F32)
        for kv in range(kvl):
            acc = acc + jnp.where(kv_of == kv, wide[:, kv * HEAD_DIM:(kv + 1) * HEAD_DIM], 0.0)
        l_hi = l.astype(BF16).astype(F32)
        at = rem(hrow + b * heads, rv)
        stat = jnp.where(lane_h == at, m, jnp.where(
            lane_h == at + rp, l_hi, jnp.where(lane_h == at + 2 * rp, l - l_hi, 0.0)))
        h0 = 0
        while h0 < heads:
            p, k0 = divmod(b * heads + h0, rv)
            count = min(rv - k0, heads - h0)
            pk[p * rp + k0:p * rp + k0 + count, :] = acc[h0:h0 + count]
            sk[p * rp + k0:p * rp + k0 + count, :] = stat[h0:h0 + count]
            h0 += count
    for p in range(n_seq):
        pk[p * rp + rv:p * rp + rv + 1, :] = jnp.sum(sk[p * rp:(p + 1) * rp, :], axis=0, keepdims=True)
    for p in range(n_seq):
        send1[p] = pk[p * rp:(p + 1) * rp, :].astype(BF16)
    recv1[me] = send1[me]
    for k in range(1, n_seq):
        started.append(send(send1.at[to_seq[k]], recv1.at[me], ss1.at[k], rs1.at[k], {"seq": to_seq[k]}))
    for k in range(1, n_seq):
        pltpu.make_async_remote_copy(
            send1.at[to_seq[k]], recv1.at[from_seq[k]], ss1.at[k], rs1.at[k],
            device_id={"seq": to_seq[k]}, device_id_type=MESH).wait_recv()

    for p in range(n_seq):
        sk[p * rp:(p + 1) * rp, :] = recv1[p].astype(F32)
    stats = sk[pl.ds(rv, n_seq, stride=rp), :]
    fade = jnp.exp(stats - jnp.max(stats, axis=0, keepdims=True))
    sums = pltpu.roll(stats, LANES - rp, 1) + pltpu.roll(stats, LANES - 2 * rp, 1)
    den = jnp.sum(sums * fade, axis=0, keepdims=True)
    share = jnp.where(den > 0.0, fade / jnp.where(den > 0.0, den, 1.0), 0.0)
    same = (iota((rp, LANES), 1) == iota((rp, LANES), 0)) & (iota((rp, LANES), 0) < rv)
    att = jnp.zeros((rp, HEAD_DIM), F32)
    for p in range(n_seq):
        col = jnp.sum(jnp.where(same, share[p:p + 1, :], 0.0), axis=1, keepdims=True)
        att = att + sk[p * rp:(p + 1) * rp, :] * col
    buf2[me] = att.astype(BF16)
    started += spread(buf2, ss2, rs2, "seq", me, to_seq)
    for c in small:
        c.wait()
    ow_copy.wait()
    collect(buf2, ss2, rs2, "seq", me, to_seq, from_seq)

    rows = dot(unpk[...], jnp.concatenate([buf2[p] for p in range(n_seq)], axis=0))
    att_all = jnp.concatenate([rows[h * bp:(h + 1) * bp] for h in range(heads)], axis=1).astype(BF16)
    part = dot(att_all, ow[...])
    hidden = hid[...].astype(F32)
    rowc = iota((bp, width), 0)
    for t in range(toks):
        part = part + jnp.where(rowc == my_e * toks + t, hidden[t:t + 1, :], 0.0)
    buf3[my_e] = part
    started += spread(buf3, ss3, rs3, "exp", my_e, to_exp)
    collect(buf3, ss3, rs3, "exp", my_e, to_exp, from_exp)
    residual = functools.reduce(lambda a, b: a + b, [buf3[e] for e in range(n_exp)])
    gained = residual * gain[...]
    top = gained.astype(BF16)
    buf4[me] = top
    started += spread(buf4, ss4, rs4, "seq", me, to_seq)

    low = (gained - top.astype(F32)).astype(BF16)
    both = dot_nt(jnp.concatenate([top.astype(F32), low.astype(F32)], axis=0).astype(BF16), rt[...])
    pad = jnp.zeros((bp, LANES - n_experts), F32)
    logit = jnp.concatenate([both[:bp] + both[bp:], pad], axis=1)
    square = jnp.sum(residual * residual, axis=1, keepdims=True)
    st = jnp.where(lane == n_experts, square, logit)
    st_hi = st.astype(BF16).astype(F32)
    half = LANES // 2
    st4[me] = (st_hi + pltpu.roll(st - st_hi, half, 1)).astype(BF16)
    started += spread(st4, sst, rst, "seq", me, to_seq)
    own = []
    for t in range(toks):
        own.append(jnp.sum(jnp.where(rowc == my_e * toks + t, residual, 0.0), axis=0, keepdims=True))
    collect(idx, ssi, rsi, "exp", my_e, to_exp, from_exp)
    idv = functools.reduce(lambda a, b: a + b, [idx[e] for e in range(n_exp)]).astype(jnp.int32)
    ids = [idv[:, k:k + 1] for k in range(2)]
    rowb = iota((bp, 1), 0)
    place = rem(rowb, toks)
    keep = []
    for k in range(2):
        rank = jnp.zeros((bp, 1), jnp.int32)
        for d in range(1, toks):
            for j in range(2):
                before = pltpu.roll(idv, d, 0)[:, j:j + 1]
                rank = rank + jnp.where((place >= d) & (ids[k] == before), 1, 0)
        limit = jnp.zeros((bp, 1), jnp.int32)
        for e in range(n_experts):
            limit = limit + jnp.where(ids[k] == e, cap_ref[e], 0)
        keep.append((rank < limit) & (rowb < seqs))

    collect(buf4, ss4, rs4, "seq", me, to_seq, from_seq)
    for p in range(n_seq):
        xg[:, p * width:(p + 1) * width] = buf4[p]
    x = xg[...]

    def product(i):
        weight_wait(i)
        return dot(x, pool[i % slots])

    def refill(i):
        if i + slots < len(order):
            for c in weight_copies(i + slots):
                c.start()

    scale = None
    coef = None
    gates = {}
    hidden_of = {}
    for i, (kind, e) in enumerate(order):
        if kind == "gate":
            gates[e] = product(i)
        elif kind == "up":
            u = product(i)
            if scale is None:
                collect(st4, sst, rst, "seq", me, to_seq, from_seq)
                tot = functools.reduce(lambda a, b: a + b, [st4[p].astype(F32) for p in range(n_seq)])
                tot = tot + pltpu.roll(tot, half, 1)
                scale = lax.rsqrt(tot[:, n_experts:n_experts + 1] / model + norm_eps)
                logits = jnp.where(lane < n_experts, tot, 0.0) * scale
                chosen = [jnp.sum(jnp.where(lane == ids[k], logits, 0.0), axis=1, keepdims=True) for k in range(2)]
                coef = [jnp.where(keep[k], jax.nn.sigmoid(chosen[k] - chosen[1 - k]), 0.0) for k in range(2)]
            ge = my_e * local + e
            c = jnp.where(ids[0] == ge, coef[0], 0.0) + jnp.where(ids[1] == ge, coef[1], 0.0)
            hidden_of[e] = (jax.nn.silu(gates[e] * scale) * (u * scale) * c).astype(BF16)
        else:
            weight_wait(i)
            for j in range(model // ffl):
                cols = slice(j * ffl, (j + 1) * ffl)
                part = dot(hidden_of[e], pool[i % slots, cols, :])
                y[:, cols] = part if e == 0 else y[:, cols] + part
        refill(i)

    for e in range(n_exp):
        rows = y[e * toks:(e + 1) * toks, :].astype(BF16)
        for s in range(n_seq):
            ysend[e * n_seq + s] = rows[:, s * width:(s + 1) * width]
    yrecv[me_all] = ysend[me_all]
    for k in range(1, n):
        started.append(send(ysend.at[to_all[k]], yrecv.at[me_all], ss5.at[k], rs5.at[k], where_is(to_all[k])))
    total = jnp.concatenate(own, axis=0)
    for k in range(1, n):
        pltpu.make_async_remote_copy(
            ysend.at[to_all[k]], yrecv.at[from_all[k]], ss5.at[k], rs5.at[k],
            device_id=where_is(to_all[k]), device_id_type=MESH).wait_recv()
    for p in range(n):
        total = total + yrecv[p].astype(F32)
    o_ref[...] = total.astype(BF16)
    for c in started:
        c.wait_send()


def on_device(
    n_seq, n_exp, hidden_in, queries, key_cache, value_cache, lengths, out_weight, norm_gain,
    router, expert_ids, capacity, w_gate, w_up, w_down,
):
    seqs = queries.shape[0]
    toks, width = hidden_in.shape
    span, kv_width = key_cache.shape[1:]
    kvl = kv_width // HEAD_DIM
    heads = queries.shape[1] // HEAD_DIM
    group = heads // kvl
    bp = up(seqs, 8)
    n_experts = router.shape[1]
    model = width * n_seq
    local, _, ffl = w_gate.shape
    rv = -(-seqs * heads // n_seq)
    rp = up(rv + 1, 16)
    n = n_seq * n_exp
    fixed = 2 * (2 * seqs * span * kv_width + out_weight.size)
    spare = 7 << 18
    slots = min(3 * local, (VMEM_BYTES - fixed - spare) // (2 * model * ffl))
    vmem = pl.BlockSpec(memory_space=pltpu.VMEM)
    smem = pl.BlockSpec(memory_space=pltpu.SMEM)
    hbm = pl.BlockSpec(memory_space=pltpu.HBM)
    dma = pltpu.SemaphoreType.DMA
    return pl.pallas_call(
        functools.partial(layer_kernel, (n_seq, n_exp, seqs, toks, kvl, group, rv, rp, n_experts, slots)),
        in_specs=[smem, smem, smem] + [hbm] * 10,
        out_specs=vmem,
        out_shape=jax.ShapeDtypeStruct((toks, width), BF16),
        scratch_shapes=[
            pltpu.VMEM((toks, width), BF16),
            pltpu.VMEM(queries.shape, BF16),
            pltpu.VMEM(key_cache.shape, BF16),
            pltpu.VMEM(value_cache.shape, BF16),
            pltpu.VMEM(out_weight.shape, BF16),
            pltpu.VMEM((1, width), F32),
            pltpu.VMEM((n_experts, width), BF16),
            pltpu.VMEM((slots, model, ffl), BF16),
            pltpu.VMEM((heads * bp, HEAD_DIM), F32),
            pltpu.VMEM((n_seq * rp, HEAD_DIM), F32),
            pltpu.VMEM((n_seq * rp, HEAD_DIM), F32),
            pltpu.VMEM((heads * bp, n_seq * rp), BF16),
            pltpu.VMEM((n_seq, rp, HEAD_DIM), BF16),
            pltpu.VMEM((n_seq, rp, HEAD_DIM), BF16),
            pltpu.VMEM((n_seq, rp, HEAD_DIM), BF16),
            pltpu.VMEM((n_exp, bp, width), F32),
            pltpu.VMEM((n_exp, bp, LANES), F32),
            pltpu.VMEM((n_seq, bp, width), BF16),
            pltpu.VMEM((n_seq, bp, LANES), BF16),
            pltpu.VMEM((bp, model), BF16),
            pltpu.VMEM((bp, model), F32),
            pltpu.VMEM((n, toks, width), BF16),
            pltpu.VMEM((n, toks, width), BF16),
            dma((5,)), dma((seqs, 2)), dma((3 * local,)),
            dma((n_seq,)), dma((n_seq,)), dma((n_seq,)), dma((n_seq,)),
            dma((n_exp,)), dma((n_exp,)), dma((n_exp,)), dma((n_exp,)),
            dma((n_seq,)), dma((n_seq,)), dma((n_seq,)), dma((n_seq,)),
            dma((n,)), dma((n,)),
        ],
        compiler_params=pltpu.CompilerParams(
            collective_id=0, has_side_effects=True, vmem_limit_bytes=VMEM_BYTES),
        name="layer",
    )(
        lengths, capacity, expert_ids.T, hidden_in, queries, key_cache, value_cache, out_weight, norm_gain,
        router.T, w_gate, w_up, w_down,
    )


def solution(mesh):
    in_specs = (
        P("exp", "seq"),
        P(None, "exp"),
        P(None, "seq", "exp"),
        P(None, "seq", "exp"),
        P(),
        P("exp", "seq"),
        P("seq"),
        P("seq", None),
        P("exp", None),
        P(),
        P("exp", None, "seq"),
        P("exp", None, "seq"),
        P("exp", "seq", None),
    )
    return jax.shard_map(
        functools.partial(on_device, mesh.shape["seq"], mesh.shape["exp"]),
        mesh=mesh, in_specs=in_specs, out_specs=P("exp", "seq"), check_vma=False,
    )
```

time: 74.6 us -> 60 us (0.80)
  local copies, waits for them, and re-layouts: 10.4 us -> 1.26 us
  Pallas kernels: 63.4 us -> 58.5 us
    unnamed x13 -> x1, local copies, waits for them, and re-layouts: 6.95 us -> 1.26 us
    pallas_call x4 -> x1, Pallas kernels: 63.4 us -> 58.5 us  [on_device(): pl.pallas_call(functools.partial(layer_kernel, (n_seq, n_exp, seqs, toks,...]
    reshape x2 -> x0, local copies, waits for them, and re-layouts: 2.12 us -> none  [the longest x1 1.26 us: on_device(): norm_gain.reshape(1, width)]
    pad x2 -> x0, local copies, waits for them, and re-layouts: 1.3 us -> none  [the longest x1 0.67 us: on_device(): rt = jnp.pad(router, ((0, 0), (0, LANES - n_experts)))]
where the time goes in v1:
time: 60 us; the launch traced here: 59.8 us
  Pallas kernels  58.5 us (98%)
  local copies, waits for them, and re-layouts  1.26 us (2%)
    pallas_call x1, Pallas kernels, on_device(): pl.pallas_call(functools.partial(layer_kernel, (n_seq, n_exp, seqs, toks,...  58.5 us
    unnamed x1, local copies, waits for them, and re-layouts  1.26 us

profile of v1, /device:TPU:0, one launch (start us, length us, event | category | flops | bytes accessed | tf_op | source)
XLA Modules:
  0.0 59.8 jit_solution(462741138841007675)
XLA Ops:
  0.0 58.5 %layer.1 = bf16[3,384]{1,0:T(4,128)(2,1)} custom-call(s32[6]{0:T(128)} %len_ref.1, s32[8]{0:T(128)} %cap_ref.1, s32[2,3]{1,0:T(2,128)} %bitcast.3, bf16[3,384]{1,0:T(4,128)(2,1)} %hid_hbm.1, bf16[6,3072]{1,0:T(8,128)(2,1)} %q_hbm.1, bf16[6,512,512]{2,1,0:T(8,128)(2,1)} %k_hbm.1, bf16[6,512,512]{2,1,0:T(8,128)(2,1)} %v_hbm.1, bf16[3072,384]{1,0:T(8,128)(2,1)} %ow_hbm.1, ...), custom_call_target="tpu_custom_call" | custom-call | tf_op jit(solution)/shard_map/layer/pallas_call | solution.py:365
  58.5 1.3 %copy.15 = bf16[3,384]{1,0:T(4,128)(2,1)} copy(bf16[3,384]{1,0:T(4,128)(2,1)} %layer.1) | data formatting | bytes 4608

commit v2 on v1

v2 whole, which is shorter than its diff:
```python
import functools
import math

import jax
import jax.numpy as jnp
from jax import lax
from jax.experimental import pallas as pl
from jax.experimental.pallas import tpu as pltpu
from jax.sharding import PartitionSpec as P

MESH = pl.DeviceIdType.MESH
HEAD_DIM = 128
LANES = 128
VMEM_BYTES = 67043328
PRIORITY = 1
BATCH = 3
masked_score = -1e30
norm_eps = 1e-05
F32 = jnp.float32
BF16 = jnp.bfloat16


def up(value, step):
    return -(-value // step) * step


def iota(shape, axis):
    return lax.broadcasted_iota(jnp.int32, shape, axis)


def div(value, by):
    return lax.div(value, jnp.full_like(value, by))


def rem(value, by):
    return lax.rem(value, jnp.full_like(value, by))


def dot(a, b):
    return jnp.dot(a, b, preferred_element_type=F32)


def dot_nt(a, b):
    return lax.dot_general(a, b, (((1,), (1,)), ((), ())), preferred_element_type=F32)


def partner(at, step, count):
    if count & (count - 1):
        return lax.rem(at + step, count)
    bit = 1
    out = at
    while bit < count:
        if step & bit:
            out = out + bit * (1 - 2 * lax.rem(lax.div(at, bit), 2))
        bit *= 2
    return out


def ring_of(axis, count):
    me = lax.axis_index(axis)
    return me, [partner(me, k, count) for k in range(count)]


def layer_kernel(
    dims, len_hbm, cap_hbm, ids_hbm, hid_hbm, q_hbm, k_hbm, v_hbm, ow_hbm, gain_hbm, rt_hbm, wg_hbm, wu_hbm, wd_hbm,
    o_ref,
    len_ref, cap_ref, ids_ref, hid, qv, kbuf, vbuf, ow, gain, rt, pool,
    qs, pk, sk, unpk, send1, recv1, buf2, buf3, idx, buf4, st4, gu, ysend, yrecv,
    in_sem, kv_sem, w_sem, sem1, sem2, sem3, semi, sem4, sems, sem5,
):
    n_seq, n_exp, seqs, toks, kvl, group, rv, rp, n_experts, slots = dims
    heads = kvl * group
    span = kbuf.shape[1]
    bp = gu.shape[1]
    model, ffl = pool.shape[1:]
    width = model // n_seq
    local = wg_hbm.shape[0]
    n = n_seq * n_exp
    chunks = 2 * local
    kc = model // chunks
    in_chunk = n_seq // chunks
    cols = model // local
    in_block = n_seq // local
    me, to_seq = ring_of("seq", n_seq)
    my_e, to_exp = ring_of("exp", n_exp)
    me_all = my_e * n_seq + me
    to_all = [lax.rem(me_all + k, n) for k in range(n)]
    my_chunk, chunk_pos = lax.div(me, in_chunk), lax.rem(me, in_chunk)
    my_block, block_pos = lax.div(me, in_block), lax.rem(me, in_block)
    chunk_at = [partner(my_chunk, i, chunks) for i in range(chunks)]
    block_at = [partner(my_block, local - 1 - i, local) for i in range(local)]

    def chunk_members(i):
        return [
            (to_exp[k], chunk_at[i] * in_chunk + lax.rem(chunk_pos + r, in_chunk))
            for r in range(in_chunk) for k in range(n_exp)
        ]

    def where_is(p):
        return {"seq": lax.rem(p, n_seq), "exp": lax.div(p, n_seq)}

    q_copy = pltpu.make_async_copy(q_hbm, qv, in_sem.at[0])
    q_copy.start()
    numbers = [
        pltpu.make_async_copy(len_hbm, len_ref, in_sem.at[5]),
        pltpu.make_async_copy(cap_hbm, cap_ref, in_sem.at[6]),
        pltpu.make_async_copy(ids_hbm, ids_ref, in_sem.at[7]),
    ]
    for c in numbers:
        c.start()
    for b in range(seqs):
        pair = (
            pltpu.make_async_copy(k_hbm.at[b], kbuf.at[b], kv_sem.at[b // BATCH, 0]),
            pltpu.make_async_copy(v_hbm.at[b], vbuf.at[b], kv_sem.at[b // BATCH, 1]),
        )
        for c in pair:
            c.start(priority=0 if b < BATCH else 1)
    small = [
        pltpu.make_async_copy(hid_hbm, hid, in_sem.at[1]),
        pltpu.make_async_copy(gain_hbm, gain.at[0], in_sem.at[2]),
        pltpu.make_async_copy(rt_hbm, rt, in_sem.at[3]),
    ]
    ow_copy = pltpu.make_async_copy(ow_hbm, ow, in_sem.at[4])
    barrier = pltpu.get_barrier_semaphore()
    for k in range(1, n):
        pl.semaphore_signal(barrier, inc=1, device_id=where_is(to_all[k]), device_id_type=MESH)


    def weight_start(i):
        s = i % slots
        if i < chunks:
            rows = pl.ds(pl.multiple_of(chunk_at[i] * kc, kc), kc)
            for e in range(local):
                for half, w in enumerate((wg_hbm, wu_hbm)):
                    at = (2 * e + half) * kc
                    pltpu.make_async_copy(w.at[e, rows, :], pool.at[s, pl.ds(at, kc), :], w_sem.at[i]).start(priority=PRIORITY)
        else:
            for j in range(cols // ffl):
                part = pl.ds(pl.multiple_of(block_at[i - chunks] * cols + j * ffl, ffl), ffl)
                for e in range(local):
                    at = (j * local + e) * ffl
                    pltpu.make_async_copy(wd_hbm.at[e, :, part], pool.at[s, pl.ds(at, ffl), :], w_sem.at[i]).start(priority=PRIORITY)

    def weight_wait(i):
        pltpu.make_async_copy(wg_hbm.at[0], pool.at[i % slots], w_sem.at[i]).wait()

    loads = chunks + local

    def refill(i):
        if i + slots < loads:
            weight_start(i + slots)

    ahead = min(slots, loads)
    turn = min(5, ahead)
    waves = [range(turn), range(turn, ahead)]

    pk[...] = jnp.zeros_like(pk)
    sk[...] = jnp.zeros_like(sk)
    qs[...] = jnp.zeros_like(qs)
    row = iota((heads * bp, 1), 0)
    row_b = rem(row, bp)
    want = jnp.where(row_b < seqs, row_b * heads + div(row, bp), -3)
    slot = iota((1, n_seq * rp), 1)
    slot_k = rem(slot, rp)
    have = jnp.where(slot_k < rv, div(slot, rp) * rv + slot_k, -2)
    unpk[...] = (want == have).astype(F32).astype(BF16)

    q_copy.wait()
    for h in range(heads):
        qs[h * bp:h * bp + seqs, :] = qv[:, h * HEAD_DIM:(h + 1) * HEAD_DIM].astype(F32)

    rowl = iota((bp, LANES), 0)
    lane = iota((bp, LANES), 1)
    for c in numbers:
        c.wait()
    mine = jnp.zeros((bp, LANES), F32)
    for t in range(toks):
        for k in range(2):
            mine = mine + jnp.where((rowl == my_e * toks + t) & (lane == k), ids_ref[k, t].astype(F32), 0.0)
    idx[my_e] = mine

    def send(src, dst, send_sem, recv_sem, device):
        c = pltpu.make_async_remote_copy(src, dst, send_sem, recv_sem, device_id=device, device_id_type=MESH)
        c.start()
        return c

    peer = {"seq": to_seq[1 % n_seq], "exp": to_exp[1 % n_exp]}

    def whole(buf, count, sems):
        part = buf.at[pl.ds(0, count)]
        return pltpu.make_async_remote_copy(part, part, sems.at[0], sems.at[1], device_id=peer, device_id_type=MESH)

    def spread(buf, sems, axis, mine_at, to):
        for k in reversed(range(1, len(to))):
            send(buf.at[mine_at], buf.at[mine_at], sems.at[0], sems.at[1], {axis: to[k]})
        return whole(buf, len(to) - 1, sems)

    first = me * span
    pos = iota((heads, span), 1) + first
    hrow = iota((heads, 1), 0)
    kv_of = div(hrow, group)
    diag = div(iota((heads, kvl * HEAD_DIM), 1), HEAD_DIM) == kv_of
    lane_h = iota((heads, LANES), 1)

    def attend(batch):
        scores = []
        for b in batch:
            qb = qs[pl.ds(b, heads, stride=bp), :]
            qd = jnp.where(diag, jnp.concatenate([qb] * kvl, axis=1), 0.0).astype(BF16)
            scores.append(dot_nt(qd, kbuf[b]) * (1.0 / math.sqrt(HEAD_DIM)))
        weights = []
        for b, s in zip(batch, scores):
            live = pos < len_ref[b]
            m = jnp.max(jnp.where(live, s, masked_score), axis=1, keepdims=True).astype(BF16).astype(F32)
            w = jnp.where(live, jnp.exp(s - m), 0.0)
            weights.append((m, jnp.sum(w, axis=1, keepdims=True), w.astype(BF16)))
        for b, (m, l, w) in zip(batch, weights):
            wide = dot(w, vbuf[b])
            acc = jnp.zeros((heads, HEAD_DIM), F32)
            for kv in range(kvl):
                acc = acc + jnp.where(kv_of == kv, wide[:, kv * HEAD_DIM:(kv + 1) * HEAD_DIM], 0.0)
            l_hi = l.astype(BF16).astype(F32)
            at = rem(hrow + b * heads, rv)
            stat = jnp.where(lane_h == at, m, jnp.where(
                lane_h == at + rp, l_hi, jnp.where(lane_h == at + 2 * rp, l - l_hi, 0.0)))
            h0 = 0
            while h0 < heads:
                p, k0 = divmod(b * heads + h0, rv)
                count = min(rv - k0, heads - h0)
                pk[p * rp + k0:p * rp + k0 + count, :] = acc[h0:h0 + count]
                sk[p * rp + k0:p * rp + k0 + count, :] = stat[h0:h0 + count]
                h0 += count

    per = BATCH
    for b0 in range(0, seqs, per):
        batch = range(b0, min(b0 + per, seqs))
        some = pl.ds(b0, len(batch))
        pltpu.make_async_copy(k_hbm.at[some], kbuf.at[some], kv_sem.at[b0 // BATCH, 0]).wait()
        pltpu.make_async_copy(v_hbm.at[some], vbuf.at[some], kv_sem.at[b0 // BATCH, 1]).wait()
        if b0 + per >= seqs:
            for c in small + [ow_copy]:
                c.start()
            for i in waves[0]:
                weight_start(i)
        attend(batch)
    for p in range(n_seq):
        pk[p * rp + rv:p * rp + rv + 1, :] = jnp.sum(sk[p * rp:(p + 1) * rp, :], axis=0, keepdims=True)
    for p in range(n_seq):
        send1[p] = pk[p * rp:(p + 1) * rp, :].astype(BF16)
    recv1[me] = send1[me]
    pl.semaphore_wait(barrier, n - 1)
    for k in reversed(range(1, n_seq)):
        send(send1.at[to_seq[k]], recv1.at[me], sem1.at[0], sem1.at[1], {"seq": to_seq[k]})
    out1 = whole(recv1, n_seq - 1, sem1)
    outi = spread(idx, semi, "exp", my_e, to_exp)
    out1.wait_recv()
    for i in waves[1]:
        weight_start(i)
    for p in range(n_seq):
        sk[p * rp:(p + 1) * rp, :] = recv1[p].astype(F32)
    stats = sk[pl.ds(rv, n_seq, stride=rp), :]
    fade = jnp.exp(stats - jnp.max(stats, axis=0, keepdims=True))
    sums = pltpu.roll(stats, LANES - rp, 1) + pltpu.roll(stats, LANES - 2 * rp, 1)
    den = jnp.sum(sums * fade, axis=0, keepdims=True)
    share = jnp.where(den > 0.0, fade / jnp.where(den > 0.0, den, 1.0), 0.0)
    same = (iota((rp, LANES), 1) == iota((rp, LANES), 0)) & (iota((rp, LANES), 0) < rv)
    att = jnp.zeros((rp, HEAD_DIM), F32)
    for p in range(n_seq):
        col = jnp.sum(jnp.where(same, share[p:p + 1, :], 0.0), axis=1, keepdims=True)
        att = att + sk[p * rp:(p + 1) * rp, :] * col
    buf2[me] = att.astype(BF16)
    out2 = spread(buf2, sem2, "seq", me, to_seq)
    for c in small:
        c.wait()
    ow_copy.wait()
    outi.wait_recv()
    idv = functools.reduce(lambda a, b: a + b, [idx[e] for e in range(n_exp)]).astype(jnp.int32)
    ids = [idv[:, k:k + 1] for k in range(2)]
    rowb = iota((bp, 1), 0)
    place = rem(rowb, toks)
    keep = []
    for k in range(2):
        rank = jnp.zeros((bp, 1), jnp.int32)
        for d in range(1, toks):
            for j in range(2):
                before = pltpu.roll(idv, d, 0)[:, j:j + 1]
                rank = rank + jnp.where((place >= d) & (ids[k] == before), 1, 0)
        limit = jnp.zeros((bp, 1), jnp.int32)
        for e in range(n_experts):
            limit = limit + jnp.where(ids[k] == e, cap_ref[e], 0)
        keep.append((rank < limit) & (rowb < seqs))
    out2.wait_recv()

    rows = dot(unpk[...], jnp.concatenate([buf2[p] for p in range(n_seq)], axis=0))
    att_all = jnp.concatenate([rows[h * bp:(h + 1) * bp] for h in range(heads)], axis=1).astype(BF16)
    part = dot(att_all, ow[...])
    hidden = hid[...].astype(F32)
    rowc = iota((bp, width), 0)
    for t in range(toks):
        part = part + jnp.where(rowc == my_e * toks + t, hidden[t:t + 1, :], 0.0)
    here = me * n_exp + my_e
    buf4[here] = (part * gain[...]).astype(BF16)
    buf3[my_e] = part
    group_size = in_chunk * n_exp
    both_ways = chunks & (chunks - 1) == 0
    for i in range(chunks):
        for at, (to_e, to_s) in enumerate(chunk_members(i)):
            if i or at:
                back = (in_chunk - at // n_exp) % in_chunk * n_exp + (n_exp - at % n_exp) % n_exp
                arrival = group_size + (i if both_ways else chunks - i) if i else back
                send(buf4.at[here], buf4.at[here], sem4.at[0], sem4.at[arrival], {"seq": to_s, "exp": to_e})
        if i == 0:
            out3 = spread(buf3, sem3, "exp", my_e, to_exp)
    out4 = pltpu.make_async_remote_copy(
        buf4.at[pl.ds(0, n - 1)], buf4.at[pl.ds(0, n - 1)], sem4.at[0], sem4.at[1], device_id=peer, device_id_type=MESH)

    half = LANES // 2

    for i in range(chunks):
        if i:
            part = buf4.at[pl.ds(chunk_at[i] * group_size, group_size)]
            pltpu.make_async_remote_copy(
                part, part, sem4.at[0], sem4.at[group_size + i], device_id=peer, device_id_type=MESH).wait_recv()
        else:
            for at, (of_e, of_s) in enumerate(chunk_members(0)):
                if at:
                    part = buf4.at[of_s * n_exp + of_e]
                    pltpu.make_async_remote_copy(
                        part, part, sem4.at[0], sem4.at[at], device_id=peer, device_id_type=MESH).wait_recv()
        if i == chunks - 1:
            outs.wait_recv()
            tot = functools.reduce(lambda a, b: a + b, [st4[p].astype(F32) for p in range(n_seq)])
            tot = tot + pltpu.roll(tot, half, 1)
            scale = lax.rsqrt(tot[:, n_experts:n_experts + 1] / model + norm_eps)
            logits = jnp.where(lane < n_experts, tot, 0.0) * scale
            chosen = [jnp.sum(jnp.where(lane == ids[k], logits, 0.0), axis=1, keepdims=True) for k in range(2)]
            coef = [jnp.where(keep[k], jax.nn.sigmoid(chosen[k] - chosen[1 - k]), 0.0) for k in range(2)]
        if i == 0:
            out3.wait_recv()
        weight_wait(i)
        s = i % slots
        if i == 0:
            residual = functools.reduce(lambda a, b: a + b, [buf3[e] for e in range(n_exp)])
            gained = residual * gain[...]
            top = gained.astype(BF16).astype(F32)
            both = dot_nt(jnp.concatenate([top, gained - top], axis=0).astype(BF16), rt[...])
            pad = jnp.zeros((bp, LANES - n_experts), F32)
            logit = jnp.concatenate([both[:bp] + both[bp:], pad], axis=1)
            square = jnp.sum(residual * residual, axis=1, keepdims=True)
            st = jnp.where(lane == n_experts, square, logit)
            st_hi = st.astype(BF16).astype(F32)
            st4[me] = (st_hi + pltpu.roll(st - st_hi, half, 1)).astype(BF16)
            own = jnp.concatenate([
                jnp.sum(jnp.where(rowc == my_e * toks + t, residual, 0.0), axis=0, keepdims=True) for t in range(toks)
            ], axis=0)
        pieces = []
        for r in range(in_chunk):
            at = chunk_at[i] * in_chunk + r
            pieces.append(functools.reduce(lambda a, b: a + b, [buf4[at * n_exp + e].astype(F32) for e in range(n_exp)]))
        x = jnp.concatenate(pieces, axis=1).astype(BF16)
        for m in range(chunks):
            part = dot(x, pool[s, m * kc:(m + 1) * kc, :])
            gu[m] = part if i == 0 else gu[m] + part
        refill(i)
        if i == 0:
            outs = spread(st4, sems, "seq", me, to_seq)

    inner = []
    for e in range(local):
        ge = my_e * local + e
        c = jnp.where(ids[0] == ge, coef[0], 0.0) + jnp.where(ids[1] == ge, coef[1], 0.0)
        inner.append(jax.nn.silu(gu[2 * e] * scale) * (gu[2 * e + 1] * scale) * c)
    inner = jnp.concatenate(inner, axis=1).astype(BF16)

    for i in range(local):
        weight_wait(chunks + i)
        s = (chunks + i) % slots
        deep = local * ffl
        y = jnp.concatenate(
            [dot(inner, pool[s, j * deep:(j + 1) * deep, :]) for j in range(cols // ffl)], axis=1).astype(BF16)
        base = block_at[i] * in_block
        for e in range(n_exp):
            for r in range(in_block):
                ysend[e * n_seq + base + r] = y[e * toks:(e + 1) * toks, r * width:(r + 1) * width]
        refill(chunks + i)
        for r in range(in_block):
            for k in range(n_exp):
                to_s = base + lax.rem(block_pos + r, in_block)
                to = to_exp[k] * n_seq + to_s
                if i == local - 1 and r == 0 and k == 0:
                    yrecv[me_all] = ysend[me_all]
                else:
                    send(ysend.at[to], yrecv.at[me_all], sem5.at[0], sem5.at[1], {"seq": to_s, "exp": to_exp[k]})
    out5 = whole(yrecv, n - 1, sem5)
    for c in (out1, outi, out2, out3, out4, outs):
        c.wait_send()
    total = own
    out5.wait_recv()
    for p in range(n):
        total = total + yrecv[p].astype(F32)
    o_ref[...] = total.astype(BF16)
    out5.wait_send()


def on_device(
    n_seq, n_exp, hidden_in, queries, key_cache, value_cache, lengths, out_weight, norm_gain,
    router, expert_ids, capacity, w_gate, w_up, w_down,
):
    seqs = queries.shape[0]
    toks, width = hidden_in.shape
    span, kv_width = key_cache.shape[1:]
    kvl = kv_width // HEAD_DIM
    heads = queries.shape[1] // HEAD_DIM
    group = heads // kvl
    bp = up(seqs, 8)
    n_experts = router.shape[1]
    model = width * n_seq
    local, _, ffl = w_gate.shape
    rv = -(-seqs * heads // n_seq)
    rp = up(rv + 1, 16)
    n = n_seq * n_exp
    fixed = 2 * (2 * seqs * span * kv_width + out_weight.size)
    spare = 7 << 18
    slots = min(3 * local, (VMEM_BYTES - fixed - spare) // (2 * model * ffl))
    vmem = pl.BlockSpec(memory_space=pltpu.VMEM)
    hbm = pl.BlockSpec(memory_space=pltpu.HBM)
    dma = pltpu.SemaphoreType.DMA
    return pl.pallas_call(
        functools.partial(layer_kernel, (n_seq, n_exp, seqs, toks, kvl, group, rv, rp, n_experts, slots)),
        in_specs=[hbm] * 13,
        out_specs=vmem,
        out_shape=jax.ShapeDtypeStruct((toks, width), BF16),
        scratch_shapes=[
            pltpu.SMEM(lengths.shape, jnp.int32),
            pltpu.SMEM(capacity.shape, jnp.int32),
            pltpu.SMEM(expert_ids.shape[::-1], jnp.int32),
            pltpu.VMEM((toks, width), BF16),
            pltpu.VMEM(queries.shape, BF16),
            pltpu.VMEM(key_cache.shape, BF16),
            pltpu.VMEM(value_cache.shape, BF16),
            pltpu.VMEM(out_weight.shape, BF16),
            pltpu.VMEM((1, width), F32),
            pltpu.VMEM((n_experts, width), BF16),
            pltpu.VMEM((slots, model, ffl), BF16),
            pltpu.VMEM((heads * bp, HEAD_DIM), F32),
            pltpu.VMEM((n_seq * rp, HEAD_DIM), F32),
            pltpu.VMEM((n_seq * rp, HEAD_DIM), F32),
            pltpu.VMEM((heads * bp, n_seq * rp), BF16),
            pltpu.VMEM((n_seq, rp, HEAD_DIM), BF16),
            pltpu.VMEM((n_seq, rp, HEAD_DIM), BF16),
            pltpu.VMEM((n_seq, rp, HEAD_DIM), BF16),
            pltpu.VMEM((n_exp, bp, width), F32),
            pltpu.VMEM((n_exp, bp, LANES), F32),
            pltpu.VMEM((n, bp, width), BF16),
            pltpu.VMEM((n_seq, bp, LANES), BF16),
            pltpu.VMEM((2 * local, bp, ffl), F32),
            pltpu.VMEM((n, toks, width), BF16),
            pltpu.VMEM((n, toks, width), BF16),
            dma((8,)), dma((-(-seqs // BATCH), 2)), dma((3 * local,)),
            dma((2,)), dma((2,)), dma((2,)), dma((2,)), dma((n // (2 * local) + 2 * local,)), dma((2,)), dma((2,)),
        ],
        compiler_params=pltpu.CompilerParams(
            collective_id=0, has_side_effects=True, vmem_limit_bytes=VMEM_BYTES),
        name="layer",
    )(
        lengths, capacity, expert_ids.T, hidden_in, queries, key_cache, value_cache, out_weight, norm_gain,
        router.T, w_gate, w_up, w_down,
    )


def solution(mesh):
    in_specs = (
        P("exp", "seq"),
        P(None, "exp"),
        P(None, "seq", "exp"),
        P(None, "seq", "exp"),
        P(),
        P("exp", "seq"),
        P("seq"),
        P("seq", None),
        P("exp", None),
        P(),
        P("exp", None, "seq"),
        P("exp", None, "seq"),
        P("exp", "seq", None),
    )
    return jax.shard_map(
        functools.partial(on_device, mesh.shape["seq"], mesh.shape["exp"]),
        mesh=mesh, in_specs=in_specs, out_specs=P("exp", "seq"), check_vma=False,
    )
```

time: 60 us -> 35.4 us (0.59)
  Pallas kernels: 58.5 us -> 33.9 us
    pallas_call x1, Pallas kernels: 58.5 us -> 33.9 us  [on_device(): pl.pallas_call(functools.partial(layer_kernel, (n_seq, n_exp, seqs, toks,...]
where the time goes in v2:
time: 35.4 us; the launch traced here: 35.2 us
  Pallas kernels  33.9 us (96%)
  local copies, waits for them, and re-layouts  1.26 us (4%)
    pallas_call x1, Pallas kernels, on_device(): pl.pallas_call(functools.partial(layer_kernel, (n_seq, n_exp, seqs, toks,...  33.9 us
    unnamed x1, local copies, waits for them, and re-layouts  1.26 us

profile of v2, /device:TPU:0, one launch (start us, length us, event | category | flops | bytes accessed | tf_op | source)
XLA Modules:
  0.0 35.2 jit_solution(11040835914766424517)
XLA Ops:
  0.0 33.9 %layer.1 = bf16[3,384]{1,0:T(4,128)(2,1)} custom-call(s32[6]{0:T(128)} %len_hbm.1, s32[8]{0:T(128)} %cap_hbm.1, s32[2,3]{1,0:T(2,128)} %bitcast.3, bf16[3,384]{1,0:T(4,128)(2,1)} %hid_hbm.1, bf16[6,3072]{1,0:T(8,128)(2,1)} %q_hbm.1, bf16[6,512,512]{2,1,0:T(8,128)(2,1)} %k_hbm.1, bf16[6,512,512]{2,1,0:T(8,128)(2,1)} %v_hbm.1, bf16[3072,384]{1,0:T(8,128)(2,1)} %ow_hbm.1, ...), custom_call_target="tpu_custom_call" | custom-call | tf_op jit(solution)/shard_map/layer/pallas_call | solution.py:428
  33.9 1.3 %copy.15 = bf16[3,384]{1,0:T(4,128)(2,1)} copy(bf16[3,384]{1,0:T(4,128)(2,1)} %layer.1) | data formatting | bytes 4608

commit v3 on v2

--- a/solution.py
+++ b/solution.py
@@ -11,7 +11,7 @@
 MESH = pl.DeviceIdType.MESH
 HEAD_DIM = 128
 LANES = 128
-VMEM_BYTES = 67043328
+VMEM_BYTES = 67043328 - (1 << 19)
 PRIORITY = 1
 BATCH = 3
 masked_score = -1e30
@@ -429,7 +429,7 @@
         functools.partial(layer_kernel, (n_seq, n_exp, seqs, toks, kvl, group, rv, rp, n_experts, slots)),
         in_specs=[hbm] * 13,
         out_specs=vmem,
-        out_shape=jax.ShapeDtypeStruct((toks, width), BF16),
+        out_shape=pltpu.VMEM((toks, width), BF16),
         scratch_shapes=[
             pltpu.SMEM(lengths.shape, jnp.int32),
             pltpu.SMEM(capacity.shape, jnp.int32),

time: 35.4 us -> 34.1 us (0.963)
  local copies, waits for them, and re-layouts: 1.26 us -> 0.58 us
  Pallas kernels: 33.9 us -> 33.3 us
    unnamed x1, local copies, waits for them, and re-layouts: 1.26 us -> 0.58 us
    pallas_call x1, Pallas kernels: 33.9 us -> 33.3 us  [on_device(): pl.pallas_call(functools.partial(layer_kernel, (n_seq, n_exp, seqs, toks,...]
where the time goes in v3:
time: 34.1 us; the launch traced here: 33.9 us
  Pallas kernels  33.3 us (98%)
  local copies, waits for them, and re-layouts  0.58 us (2%)
    pallas_call x1, Pallas kernels, on_device(): pl.pallas_call(functools.partial(layer_kernel, (n_seq, n_exp, seqs, toks,...  33.3 us

profile of v3, /device:TPU:0, one launch (start us, length us, event | category | flops | bytes accessed | tf_op | source)
XLA Modules:
  0.0 33.9 jit_solution(18353460816984902890)
XLA Ops:
  0.0 33.3 %layer.1 = bf16[3,384]{1,0:T(4,128)(2,1)S(1)} custom-call(s32[6]{0:T(128)} %len_hbm.1, s32[8]{0:T(128)} %cap_hbm.1, s32[2,3]{1,0:T(2,128)} %bitcast.3, bf16[3,384]{1,0:T(4,128)(2,1)} %hid_hbm.1, bf16[6,3072]{1,0:T(8,128)(2,1)} %q_hbm.1, bf16[6,512,512]{2,1,0:T(8,128)(2,1)} %k_hbm.1, bf16[6,512,512]{2,1,0:T(8,128)(2,1)} %v_hbm.1, bf16[3072,384]{1,0:T(8,128)(2,1)} %ow_hbm.1, ...), custom_call_target="tpu_custom_call" | custom-call | tf_op jit(solution)/shard_map/layer/pallas_call | solution.py:428
  33.3 0.6 %copy.15 = bf16[3,384]{1,0:T(4,128)(2,1)} copy(bf16[3,384]{1,0:T(4,128)(2,1)S(1)} %layer.1) | data formatting | bytes 4608
